TPU v7x, 32 devices: a whole 2x2x4 slice. The times are simulated.
32 devices in a mesh: grp: 8 (over z, y), col: 4 (over x, core).
Axes of the slice: x: 2, y: 2, z: 4, core: 2. Of those that a mesh axis runs over, the one named last changes fastest.
Arguments:
- features: bfloat16 [65536, 256], P(('grp', 'col')), may hold values from -6 to 6
- adj_tiles: bfloat16 [1536, 256, 256], P('grp'), may hold values from 0 to 1.5
- block_pairs: int32 [8, 192, 2], P('grp'), may hold values from 0 to 31, as said below
- tile_count: int32 [8], P('grp'), may hold values from 32 to 192, as said below
- degree: int32 [65536], P('grp'), may hold values from 1 to 769
- labels: int32 [65536], P(('grp', 'col')), may hold values from 0 to 63
- loss_mask: int32 [65536], P(('grp', 'col')), may hold values from 0 to 1
- slot_piece: int32 [8, 79], replicated, may hold values from -1 to 416, as said below
- master: float32 [632, 2, 256], P('grp', None, 'col'), may hold values from -4 to 4
- moment_one: float32 [632, 2, 256], P('grp', None, 'col'), may hold values from -0.125 to 0.125
- moment_two: float32 [632, 2, 256], P('grp', None, 'col'), may hold values from 3.0517579e-06 to 0.00030517578
Outputs:
- mean_loss: float32 [], replicated
- new_master: float32 [632, 2, 256], P('grp', None, 'col')
- new_moment_one: float32 [632, 2, 256], P('grp', None, 'col')
- new_moment_two: float32 [632, 2, 256], P('grp', None, 'col')
- new_weights: bfloat16 [632, 2, 256], P('grp', None, 'col')
Inputs may be any that keep to these rules, and one draw needn't show every extreme that they name: `block_pairs`: of each group, the first tile_count entries are distinct pairs of blocks and include every diagonal pair (r, r); later entries are padding. `tile_count`: some group has 192 live tiles in every draw. `slot_piece`: each piece 0 to 416 sits in exactly one slot; a group holds at most 79 pieces, and some group holds 79 in every draw.
All inputs are finite; a program needn't handle non-finite values.
Results may differ from a plain program's by a relative error of at most 0.0079.
Values may be sent and summed in bfloat16 or wider, within the bound.
A program may use at most 128 MiB of HBM per device.

v0:
```python
import jax
import jax.numpy as jnp
from jax import lax
from jax.sharding import PartitionSpec as P

F = 256
HID = 256
CLS = 64
B = 256
PR = 2
STEP = 7
PROWS = 834
PIECES = 417
learn_rate = 0.01
beta_one = 0.5
beta_two = 0.5
adam_epsilon = 1e-08
decay_rate = 0.1


def contract_rows(left, right):
    return lax.dot_general(
        left, right, (((0,), (0,)), ((), ())), preferred_element_type=jnp.float32
    )


def contract_cols(left, right):
    return lax.dot_general(
        left, right, (((1,), (1,)), ((), ())), preferred_element_type=jnp.float32
    )


def body(
    features,
    adj_tiles,
    block_pairs,
    tile_count,
    degree,
    labels,
    loss_mask,
    slot_piece,
    master,
    moment_one,
    moment_two,
):
    col_count = lax.axis_size("col")
    grp_count = lax.axis_size("grp")
    col_index = lax.axis_index("col")
    grp_index = lax.axis_index("grp")
    node_rows = features.shape[0]
    group_nodes = degree.shape[0]
    block_count = group_nodes // B
    tile_slots = adj_tiles.shape[0]
    slot_width = slot_piece.shape[1]
    col_width = master.shape[2]
    own_slots = master.astype(jnp.bfloat16)[None]
    gathered = lax.all_gather(own_slots, ("grp", "col"), axis=0, tiled=True)
    slot_values = gathered.reshape(grp_count, col_count, slot_width, PR, col_width)
    slot_values = slot_values.transpose(0, 2, 3, 1, 4).reshape(
        grp_count * slot_width, PR, col_count * col_width
    )
    flat_slots = slot_piece.reshape(-1)
    positions = jnp.arange(flat_slots.shape[0], dtype=jnp.int32)
    target = jnp.where(flat_slots >= 0, flat_slots, PIECES)
    piece_slot = jnp.zeros((PIECES + 1,), jnp.int32).at[target].set(positions)[:PIECES]
    weight_table = slot_values[piece_slot].reshape(PROWS, HID)
    encoder_weight = weight_table[:F]
    self_weight = weight_table[F : F + HID]
    neigh_weight = weight_table[F + HID : F + 2 * HID]
    head_weight = weight_table[F + 2 * HID : F + 2 * HID + CLS]
    encoder_bias = weight_table[PROWS - 2].astype(jnp.float32)
    sage_bias = weight_table[PROWS - 1].astype(jnp.float32)
    mask_values = loss_mask.astype(jnp.float32)
    labelled = lax.psum(jnp.sum(mask_values), ("grp", "col"))
    preact = jnp.dot(features, encoder_weight, preferred_element_type=jnp.float32) + encoder_bias
    sig_pre = jax.nn.sigmoid(preact)
    encoded = (preact * sig_pre).astype(jnp.bfloat16)
    enc_columns = lax.all_to_all(encoded, "col", split_axis=1, concat_axis=0, tiled=True)
    pairs = block_pairs[0]
    row_blocks = pairs[:, 0]
    col_blocks = pairs[:, 1]
    live_tiles = jnp.arange(tile_slots, dtype=jnp.int32) < tile_count[0]
    block_ids = jnp.arange(block_count, dtype=jnp.int32)
    row_places = ((row_blocks[None, :] == block_ids[:, None]) & live_tiles[None, :]).astype(
        jnp.float32
    )
    picked = enc_columns.reshape(block_count, B, -1)[col_blocks]
    products = jnp.einsum("tij,tjc->tic", adj_tiles, picked, preferred_element_type=jnp.float32)
    block_sums = jnp.einsum("rt,tic->ric", row_places, products, precision=lax.Precision.HIGHEST)
    degree_values = degree.astype(jnp.float32)
    mean_columns = (block_sums.reshape(group_nodes, -1) / degree_values[:, None]).astype(
        jnp.bfloat16
    )
    neigh_mean = lax.all_to_all(mean_columns, "col", split_axis=0, concat_axis=1, tiled=True)
    sage_pre = (
        jnp.dot(encoded, self_weight, preferred_element_type=jnp.float32)
        + jnp.dot(neigh_mean, neigh_weight, preferred_element_type=jnp.float32)
        + sage_bias
    )
    sig_sage = jax.nn.sigmoid(sage_pre)
    hidden = (sage_pre * sig_sage).astype(jnp.bfloat16)
    logits = contract_cols(hidden, head_weight)
    row_max = jnp.max(logits, axis=1, keepdims=True)
    log_total = row_max[:, 0] + jnp.log(jnp.sum(jnp.exp(logits - row_max), axis=1))
    label_hot = (labels[:, None] == jnp.arange(CLS, dtype=jnp.int32)[None, :]).astype(jnp.float32)
    target_logit = jnp.sum(logits * label_hot, axis=1)
    local_loss = jnp.sum(mask_values * (log_total - target_logit))
    probability = jnp.exp(logits - log_total[:, None])
    logit_grad = ((probability - label_hot) * mask_values[:, None] / labelled).astype(jnp.bfloat16)
    head_grad = contract_rows(logit_grad, hidden)
    hidden_grad = jnp.dot(logit_grad, head_weight, preferred_element_type=jnp.float32)
    sage_grad = (hidden_grad * sig_sage * (1.0 + sage_pre * (1.0 - sig_sage))).astype(jnp.bfloat16)
    self_grad = contract_rows(encoded, sage_grad)
    neigh_grad = contract_rows(neigh_mean, sage_grad)
    sage_bias_grad = jnp.sum(sage_grad.astype(jnp.float32), axis=0)
    self_back = contract_cols(sage_grad, self_weight)
    neigh_back = contract_cols(sage_grad, neigh_weight)
    degree_rows = lax.dynamic_slice_in_dim(degree_values, col_index * node_rows, node_rows)
    sum_grad = (neigh_back / degree_rows[:, None]).astype(jnp.bfloat16)
    grad_columns = lax.all_to_all(sum_grad, "col", split_axis=1, concat_axis=0, tiled=True)
    picked_grad = grad_columns.reshape(block_count, B, -1)[row_blocks]
    back_products = jnp.einsum(
        "tij,tic->tjc", adj_tiles, picked_grad, preferred_element_type=jnp.float32
    )
    col_places = ((col_blocks[None, :] == block_ids[:, None]) & live_tiles[None, :]).astype(
        jnp.float32
    )
    back_blocks = jnp.einsum(
        "rt,tjc->rjc", col_places, back_products, precision=lax.Precision.HIGHEST
    )
    neigh_return = lax.all_to_all(
        back_blocks.reshape(group_nodes, -1).astype(jnp.bfloat16),
        "col",
        split_axis=0,
        concat_axis=1,
        tiled=True,
    ).astype(jnp.float32)
    encoded_grad = self_back + neigh_return
    preact_grad = (encoded_grad * sig_pre * (1.0 + preact * (1.0 - sig_pre))).astype(jnp.bfloat16)
    encoder_grad = contract_rows(features, preact_grad)
    encoder_bias_grad = jnp.sum(preact_grad.astype(jnp.float32), axis=0)
    grad_table = jnp.concatenate(
        [
            encoder_grad,
            self_grad,
            neigh_grad,
            head_grad,
            encoder_bias_grad[None, :],
            sage_bias_grad[None, :],
        ],
        axis=0,
    )
    loss_total = lax.psum(local_loss, ("grp", "col"))
    mean_loss = loss_total / labelled
    group_grad = lax.psum_scatter(
        grad_table.astype(jnp.bfloat16), "col", scatter_dimension=1, tiled=True
    ).astype(jnp.float32)
    my_pieces = lax.dynamic_slice_in_dim(slot_piece, grp_index, 1, 0)[0]
    is_owned = my_pieces >= 0
    safe_pieces = jnp.where(is_owned, my_pieces, 0)
    owned_values = is_owned[:, None, None]
    total_grad = lax.psum(group_grad, "grp")
    slot_grad = jnp.where(owned_values, total_grad.reshape(PIECES, PR, -1)[safe_pieces], 0.0)
    table_rows = safe_pieces[:, None] * PR + jnp.arange(PR, dtype=jnp.int32)[None, :]
    decay_values = jnp.where(table_rows < PROWS - 2, decay_rate, 0.0)[:, :, None]
    first_moment = beta_one * moment_one + (1.0 - beta_one) * slot_grad
    second_moment = beta_two * moment_two + (1.0 - beta_two) * slot_grad * slot_grad
    first_hat = first_moment / (1.0 - beta_one**STEP)
    second_hat = second_moment / (1.0 - beta_two**STEP)
    updated = master - learn_rate * (
        first_hat / (jnp.sqrt(second_hat) + adam_epsilon) + decay_values * master
    )
    updated = jnp.where(owned_values, updated, 0.0)
    first_moment = jnp.where(owned_values, first_moment, 0.0)
    second_moment = jnp.where(owned_values, second_moment, 0.0)
    return (mean_loss, updated, first_moment, second_moment, updated.astype(jnp.bfloat16))


def solution(mesh):
    in_specs = (
        P(("grp", "col"), None),
        P("grp", None, None),
        P("grp", None, None),
        P("grp"),
        P("grp"),
        P(("grp", "col")),
        P(("grp", "col")),
        P(),
        P("grp", None, "col"),
        P("grp", None, "col"),
        P("grp", None, "col"),
    )
    out_specs = (
        P(),
        P("grp", None, "col"),
        P("grp", None, "col"),
        P("grp", None, "col"),
        P("grp", None, "col"),
    )
    return jax.shard_map(body, mesh=mesh, in_specs=in_specs, out_specs=out_specs, check_vma=False)
```

profile of v0, /device:TPU:0, one launch (start us, length us, event | category | flops | bytes accessed | tf_op | source)
XLA Modules:
  0.0 409.3 jit_solution(9063719519104682953)
XLA Ops:
  7.2 0.9 convert_element_type.70
  8.2 46.8 %all-gather = bf16[2528,2,64]{2,1,0:T(2,128)(2,1)S(1)} all-gather(bf16[79,2,64]{2,1,0:T(2,128)(2,1)S(1)} %copy.83), channel_id=2, replica_groups=mesh['grp'=8,'col'=4] {'grp','col'}, dimensions={0}, use_global_device_ids=true | all-gather | bytes 667392 | tf_op jit(solution)/shard_map/all_gather | solution.py:57
  55.0 1.1 copy.84
  56.1 0.8 reshape.171
  57.0 1.2 copy.85
  58.3 4.1 scatter_custom_fusion
  62.4 2.7 gather_fusion
  66.7 2.5 multiply_convert_fusion.1
  69.2 3.9 all-to-all-start
  73.9 13.6 %all-to-all-done = bf16[2048,4,64]{0,2,1:T(8,128)(2,1)S(1)} async-done(((bf16[2048,4,64]{0,2,1:T(8,128)(2,1)}), bf16[2048,4,64]{0,2,1:T(8,128)(2,1)S(1)}, u32[]{:S(2)}, u32[]{:S(2)}) %all-to-all-start) | async-done | bytes 1048608 | tf_op jit(solution)/shard_map/all_to_all | solution.py:78
  87.6 0.8 copy.86
  88.4 1.6 reshape.174
  89.9 1.8 copy.87
  91.8 8.0 %gather_fusion.1 = bf16[192,256,64]{1,2,0:T(8,128)(2,1)} fusion(bf16[32,256,64]{1,2,0:T(8,128)(2,1)S(1)} %copy.87, s32[1024]{0:T(1024)S(1)} %pad_clamp_fusion.2), kind=kCustom, calls=%fused_computation.1 | custom fusion | bytes 12583680 | tf_op jit(solution)/shard_map/gather | solution.py:87
  99.7 18.3 %convolution_bitcast_fusion.1 = f32[192,256,64]{1,2,0:T(8,128)} fusion(bf16[192,256,64]{1,2,0:T(8,128)(2,1)} %gather_fusion.1, bf16[192,256,256]{2,1,0:T(8,128)(2,1)} %param.12), kind=kOutput, calls=%fused_computation.10 | convolution fusion | flops 1610612736 | bytes 44040192 | tf_op jit(solution)/shard_map/tij,tjc->tic/dot_general | solution.py:88
  118.1 16.9 %fusion.2 = f32[32,256,64]{1,0,2:T(8,128)} fusion(f32[192,256,64]{1,2,0:T(8,128)} %convolution_bitcast_fusion.1, s32[192]{0:T(256)S(1)} %bitcast.95, pred[192]{0:T(512)(128)(4,1)S(1)} %iota_compare_fusion.3), kind=kOutput, calls=%fused_computation.7 | convolution fusion | flops 1207971840 | bytes 14681024 | tf_op jit(solution)/shard_map/rt,tic->ric/dot_general | solution.py:89
  134.9 2.2 reshape.175
  137.1 2.1 fusion.12
  139.3 3.6 all-to-all-start.1
  143.1 3.0 fusion.40
  146.2 11.1 %all-to-all-done.1 = bf16[4,2048,64]{1,2,0:T(8,128)(2,1)S(1)} async-done(((bf16[4,2048,64]{1,2,0:T(8,128)(2,1)}), bf16[4,2048,64]{1,2,0:T(8,128)(2,1)S(1)}, u32[]{:S(2)}, u32[]{:S(2)}) %all-to-all-start.1) | async-done | bytes 1048608 | tf_op jit(solution)/shard_map/all_to_all | solution.py:94
  157.3 3.7 multiply_convert_fusion
  161.0 1.0 copy-done.6
  163.1 37.2 %all-reduce = (f32[]{:T(128)}, f32[]{:T(128)}) all-reduce(f32[]{:T(128)} %get-tuple-element.27, f32[]{:T(128)} %get-tuple-element.28), channel_id=1, replica_groups=mesh['grp'=8,'col'=4] {'grp','col'}, use_global_device_ids=true, to_apply=%region_7.8 | all-reduce | flops 2 | bytes 16 | tf_op jit(solution)/shard_map/psum | solution.py:74
  200.4 3.4 fusion.39
  203.8 1.4 fusion.10
  205.2 3.5 all-to-all-start.2
  208.8 14.4 %all-to-all-done.2 = bf16[2048,4,64]{0,2,1:T(8,128)(2,1)S(1)} async-done(((bf16[2048,4,64]{0,2,1:T(8,128)(2,1)}), bf16[2048,4,64]{0,2,1:T(8,128)(2,1)S(1)}, u32[]{:S(2)}, u32[]{:S(2)}) %all-to-all-start.2) | async-done | bytes 1048608 | tf_op jit(solution)/shard_map/all_to_all | solution.py:120
  223.2 1.8 copy.94
  225.0 2.6 reshape.176
  227.6 1.8 copy.95
  229.4 8.0 %gather_fusion.2 = bf16[192,256,64]{1,2,0:T(8,128)(2,1)} fusion(bf16[32,256,64]{1,2,0:T(8,128)(2,1)S(1)} %copy.95, s32[1024]{0:T(1024)S(1)} %pad_clamp_fusion.1), kind=kCustom, calls=%fused_computation.2 | custom fusion | bytes 12583680 | tf_op jit(solution)/shard_map/gather | solution.py:121
  237.3 19.0 %convolution_bitcast_fusion = f32[192,256,64]{1,2,0:T(8,128)} fusion(bf16[192,256,64]{1,2,0:T(8,128)(2,1)} %gather_fusion.2, bf16[192,256,256]{2,1,0:T(8,128)(2,1)} %param.12), kind=kOutput, calls=%fused_computation.9 | convolution fusion | flops 1610612736 | bytes 44040192 | tf_op jit(solution)/shard_map/tij,tic->tjc/dot_general | solution.py:122
  256.3 16.4 %fusion.13 = bf16[32,256,64]{1,0,2:T(8,128)(2,1)} fusion(f32[192,256,64]{1,2,0:T(8,128)} %convolution_bitcast_fusion, s32[192]{0:T(256)S(1)} %bitcast.94, pred[192]{0:T(512)(128)(4,1)S(1)} %iota_compare_fusion.3), kind=kOutput, calls=%fused_computation.30 | convolution fusion | flops 1208496128 | bytes 13632448 | tf_op jit(solution)/shard_map/rt,tjc->rjc/dot_general | solution.py:128
  272.8 1.9 convert_element_type.80
  274.6 1.6 copy.97
  276.2 3.5 all-to-all-start.3
  279.8 3.2 convolution_convert_fusion.3
  283.4 1.7 convolution_convert_fusion.1
  285.1 9.0 %all-to-all-done.3 = bf16[4,2048,64]{1,2,0:T(8,128)(2,1)S(1)} async-done(((bf16[4,2048,64]{1,2,0:T(8,128)(2,1)}), bf16[4,2048,64]{1,2,0:T(8,128)(2,1)S(1)}, u32[]{:S(2)}, u32[]{:S(2)}) %all-to-all-start.3) | async-done | bytes 1048608 | tf_op jit(solution)/shard_map/all_to_all | solution.py:131
  294.4 1.3 copy-done.18
  295.7 1.2 fusion.38
  297.7 1.0 copy.110
  299.1 21.4 %reduce-scatter.4.cloned.1.call-done = bf16[64,834]{1,0:T(8,128)(2,1)} async-done(((bf16[256,834]{1,0:T(8,128)(2,1)}), bf16[64,834]{1,0:T(8,128)(2,1)}) %reduce-scatter.4.cloned.1.call-update) | async-done | bytes 106768
  320.6 1.1 copy.111
  321.7 1.0 reshape.177
  324.1 71.9 %all-reduce.3.cloned.1.call-done = f32[417,2,64]{2,1,0:T(2,128)} async-done(((f32[417,2,64]{2,1,0:T(2,128)}), f32[417,2,64]{2,1,0:T(2,128)}) %all-reduce.3.cloned.1.call-update) | async-done | bytes 213520 | tf_op jit(solution)/shard_map/psum | solution.py:162
  396.1 1.7 gather_fusion.3
  (86 shorter events, 8.5 us)
Async XLA Ops:
  7.2 59.5 %copy-start = (bf16[2048,256]{1,0:T(8,128)(2,1)S(1)}, bf16[2048,256]{1,0:T(8,128)(2,1)}, u32[]{:S(2)}) copy-start(bf16[2048,256]{1,0:T(8,128)(2,1)} %param.11) | copy-start | bytes 3145732
  55.0 3.2 copy-start.15
  65.1 4.1 %copy-start.4 = (bf16[417,2,256]{2,1,0:T(2,128)(2,1)}, bf16[417,2,256]{2,1,0:T(2,128)(2,1)S(1)}, u32[]{:S(2)}) copy-start(bf16[417,2,256]{2,1,0:T(2,128)(2,1)S(1)} %gather_fusion) | copy-start | bytes 1281028
  69.2 4.6 %copy-start.11 = (s32[8192]{0:T(1024)S(1)}, s32[8192]{0:T(1024)}, u32[]{:S(2)}) copy-start(s32[8192]{0:T(1024)} %param.15) | copy-start | bytes 98308
  69.2 4.7 %copy-start.16 = (s32[1,192,2]{1,2,0:T(2,128)S(1)}, s32[1,192,2]{1,2,0:T(2,128)}, u32[]{:S(2)}) copy-start(s32[1,192,2]{1,2,0:T(2,128)} %param.13) | copy-start | bytes 4612
  69.2 18.3 %all-to-all-start = ((bf16[2048,4,64]{0,2,1:T(8,128)(2,1)}), bf16[2048,4,64]{0,2,1:T(8,128)(2,1)S(1)}, u32[]{:S(2)}, u32[]{:S(2)}) async-start(bf16[2048,4,64]{0,2,1:T(8,128)(2,1)} %bitcast.8), calls=%async_computation | async-start | bytes 2097152 | tf_op jit(solution)/shard_map/all_to_all | solution.py:78
  73.9 13.7 %copy-start.8 = (f32[8192]{0:T(1024)}, f32[8192]{0:T(1024)S(1)}, u32[]{:S(2)}) copy-start(f32[8192]{0:T(1024)S(1)} %convert_element_type.72) | copy-start | bytes 98308
  139.2 3.8 slice-start
  139.2 3.8 copy-start.12
  139.3 18.1 %all-to-all-start.1 = ((bf16[4,2048,64]{1,2,0:T(8,128)(2,1)}), bf16[4,2048,64]{1,2,0:T(8,128)(2,1)S(1)}, u32[]{:S(2)}, u32[]{:S(2)}) async-start(bf16[4,2048,64]{1,2,0:T(8,128)(2,1)} %fusion.12), calls=%async_computation.1 | async-start | bytes 2097152 | tf_op jit(solution)/shard_map/all_to_all | solution.py:94
  142.9 14.4 %copy-start.17 = (f32[1,256]{1,0:T(1,128)S(1)}, f32[1,256]{1,0:T(1,128)}, u32[]{:S(2)}) copy-start(f32[1,256]{1,0:T(1,128)} %get-tuple-element.34) | copy-start | bytes 3076
  157.3 5.0 %copy-start.14 = (s32[2048]{0:T(1024)S(1)}, s32[2048]{0:T(1024)}, u32[]{:S(2)}) copy-start(s32[2048]{0:T(1024)} %param.16) | copy-start | bytes 24580
  161.0 1.0 copy-start.6
  162.3 41.4 %copy-start.5 = (f32[2048,64]{0,1:T(8,128)}, f32[2048,64]{0,1:T(8,128)S(1)}, u32[]{:S(2)}) copy-start(f32[2048,64]{0,1:T(8,128)S(1)} %get-tuple-element.50) | copy-start | bytes 1572868
  200.4 3.4 dynamic-slice-start
  203.8 1.5 copy-start.1
  205.2 18.0 %all-to-all-start.2 = ((bf16[2048,4,64]{0,2,1:T(8,128)(2,1)}), bf16[2048,4,64]{0,2,1:T(8,128)(2,1)S(1)}, u32[]{:S(2)}, u32[]{:S(2)}) async-start(bf16[2048,4,64]{0,2,1:T(8,128)(2,1)} %bitcast.92), calls=%async_computation.2 | async-start | bytes 2097152 | tf_op jit(solution)/shard_map/all_to_all | solution.py:120
  276.2 17.9 %all-to-all-start.3 = ((bf16[4,2048,64]{1,2,0:T(8,128)(2,1)}), bf16[4,2048,64]{1,2,0:T(8,128)(2,1)S(1)}, u32[]{:S(2)}, u32[]{:S(2)}) async-start(bf16[4,2048,64]{1,2,0:T(8,128)(2,1)} %copy.97), calls=%async_computation.3 | async-start | bytes 2097152 | tf_op jit(solution)/shard_map/all_to_all | solution.py:131
  279.7 40.9 %reduce-scatter.4.cloned.1.call-start = ((), (), s32[]{:S(2)}) async-start(), calls=%async_computation.6 | async-start | bytes 573440
  279.7 3.2 copy-start.2
  285.1 9.2 %copy-start.3 = (bf16[2048,256]{0,1:T(8,128)(2,1)S(1)}, bf16[2048,256]{0,1:T(8,128)(2,1)}, u32[]{:S(2)}) copy-start(bf16[2048,256]{0,1:T(8,128)(2,1)} %copy-done.1) | copy-start | bytes 3145732
  294.1 1.6 copy-start.18
  296.9 0.8 copy-start.13
  296.9 1.9 copy-start.7
  296.9 2.0 copy-start.9
  296.9 2.1 copy-start.10
  298.7 97.4 %all-reduce.3.cloned.1.call-start = ((), (), s32[]{:S(2)}) async-start(), calls=%async_computation.5 | async-start | bytes 854016 | tf_op jit(solution)/shard_map/psum | solution.py:162
Sparse Core Ops, SparseCore 0:
  298.8 21.7 reduce-scatter.3
  324.0 72.0 all-reduce.2
where the time goes:
time: 415 us; the launch traced here: 409 us
  waiting for transfers between devices  142 us (34%)
  matrix products  92.1 us (22%)
  blocking collectives  84 us (20%)
  local copies, waits for them, and re-layouts  53.8 us (13%)
  between operations  17.9 us (4%)
  starting transfers between devices  14.7 us (4%)
  other arithmetic  5.23 us (1%)
    psum x1, waiting for transfers between devices, body(): total_grad = lax.psum(group_grad, 'grp')  71.9 us
    all_gather x1, blocking collectives, body(): gathered = lax.all_gather(own_slots, ('grp', 'col'), axis=0, tiled=True)  46.8 us
    psum x1, blocking collectives, body(): labelled = lax.psum(jnp.sum(mask_values), ('grp', 'col'))  37.2 us
    unnamed x3, waiting for transfers between devices  21.5 us
    dot_general x1, matrix products, body(): jnp.einsum('tij,tic->tjc', adj_tiles, picked_grad, preferred_element_type...  19 us
    dot_general x1, matrix products, body(): jnp.einsum('tij,tjc->tic', adj_tiles, picked, preferred_element_type=jnp....  18.3 us
    dot_general x1, matrix products, body(): jnp.einsum('rt,tic->ric', row_places, products, precision=lax.Precision.H...  16.9 us
    dot_general x1, matrix products, body(): jnp.einsum('rt,tjc->rjc', col_places, back_products, precision=lax.Precis...  16.4 us
  transfers between devices with their start and end apart: 6, of which 6 were waited for; matrix products, arithmetic and copies ran while one was open for 2% of the time, Pallas kernels for 0%

commit v1 on v0

--- a/solution.py
+++ b/solution.py
@@ -159,7 +159,7 @@
     is_owned = my_pieces >= 0
     safe_pieces = jnp.where(is_owned, my_pieces, 0)
     owned_values = is_owned[:, None, None]
-    total_grad = lax.psum(group_grad, "grp")
+    total_grad = jnp.sum(lax.all_gather(group_grad, "grp"), axis=0)
     slot_grad = jnp.where(owned_values, total_grad.reshape(PIECES, PR, -1)[safe_pieces], 0.0)
     table_rows = safe_pieces[:, None] * PR + jnp.arange(PR, dtype=jnp.int32)[None, :]
     decay_values = jnp.where(table_rows < PROWS - 2, decay_rate, 0.0)[:, :, None]

time: 415 us -> 389 us (0.937)
  waiting for transfers between devices: 142 us -> 115 us
    psum x1 -> x0, waiting for transfers between devices: 71.9 us -> none  [body(): total_grad = lax.psum(group_grad, 'grp')]
    all_gather x0 -> x1, waiting for transfers between devices: none -> 44.7 us  [body(): total_grad = jnp.sum(lax.all_gather(group_grad, 'grp'), axis=0)]
    unnamed x47 -> x48, local copies, waits for them, and re-layouts: 7.83 us -> 8.77 us
where the time goes in v1:
time: 389 us; the launch traced here: 383 us
  waiting for transfers between devices  115 us (30%)
  matrix products  92.1 us (24%)
  blocking collectives  84 us (22%)
  local copies, waits for them, and re-layouts  53.1 us (14%)
  between operations  17.9 us (5%)
  starting transfers between devices  14.7 us (4%)
  other arithmetic  6.88 us (2%)
    all_gather x1, blocking collectives, body(): gathered = lax.all_gather(own_slots, ('grp', 'col'), axis=0, tiled=True)  46.8 us
    all_gather x1, waiting for transfers between devices, body(): total_grad = jnp.sum(lax.all_gather(group_grad, 'grp'), axis=0)  44.7 us
    psum x1, blocking collectives, body(): loss_total = lax.psum(local_loss, ('grp', 'col'))  37.2 us
    unnamed x3, waiting for transfers between devices  21.9 us
    dot_general x1, matrix products, body(): jnp.einsum('tij,tic->tjc', adj_tiles, picked_grad, preferred_element_type...  19 us
    dot_general x1, matrix products, body(): jnp.einsum('tij,tjc->tic', adj_tiles, picked, preferred_element_type=jnp....  18.3 us
    dot_general x1, matrix products, body(): jnp.einsum('rt,tic->ric', row_places, products, precision=lax.Precision.H...  16.9 us
    dot_general x1, matrix products, body(): jnp.einsum('rt,tjc->rjc', col_places, back_products, precision=lax.Precis...  16.4 us
  transfers between devices with their start and end apart: 6, of which 6 were waited for; matrix products, arithmetic and copies ran while one was open for 2% of the time, Pallas kernels for 0%

profile of v1, /device:TPU:0, one launch (start us, length us, event | category | flops | bytes accessed | tf_op | source)
XLA Modules:
  0.0 383.5 jit_solution(1021148369344006423)
XLA Ops:
  7.2 0.9 convert_element_type.68
  8.2 46.8 %all-gather = bf16[2528,2,64]{2,1,0:T(2,128)(2,1)S(1)} all-gather(bf16[79,2,64]{2,1,0:T(2,128)(2,1)S(1)} %copy.109), channel_id=2, replica_groups=mesh['grp'=8,'col'=4] {'grp','col'}, dimensions={0}, use_global_device_ids=true | all-gather | bytes 667392 | tf_op jit(solution)/shard_map/all_gather | solution.py:57
  55.0 1.1 copy.110
  56.1 0.8 reshape.171
  57.0 1.2 copy.111
  58.3 4.1 %scatter_custom_fusion = s32[418]{0:T(512)S(1)} fusion(s32[632]{0:T(1024)S(1)} %fusion.29, s32[632]{0:T(1024)S(1)} %iota.23, s32[]{:T(128)} %constant.21.clone.1), kind=kCustom, calls=%fused_computation.77 | custom fusion | bytes 1676 | tf_op jit(solution)/shard_map/scatter | solution.py:65
  62.4 2.7 gather_fusion
  66.7 2.5 multiply_convert_fusion.1
  69.2 3.9 %all-to-all-start = ((bf16[2048,4,64]{0,2,1:T(8,128)(2,1)}), bf16[2048,4,64]{0,2,1:T(8,128)(2,1)S(1)}, u32[]{:S(2)}, u32[]{:S(2)}) async-start(bf16[2048,4,64]{0,2,1:T(8,128)(2,1)} %bitcast.8), calls=%async_computation | async-start | bytes 2097152 | tf_op jit(solution)/shard_map/all_to_all | solution.py:78
  73.9 13.6 %all-to-all-done = bf16[2048,4,64]{0,2,1:T(8,128)(2,1)S(1)} async-done(((bf16[2048,4,64]{0,2,1:T(8,128)(2,1)}), bf16[2048,4,64]{0,2,1:T(8,128)(2,1)S(1)}, u32[]{:S(2)}, u32[]{:S(2)}) %all-to-all-start) | async-done | bytes 1048608 | tf_op jit(solution)/shard_map/all_to_all | solution.py:78
  87.6 0.8 copy.112
  88.4 1.6 reshape.174
  89.9 1.8 copy.113
  91.8 8.0 %gather_fusion.1 = bf16[192,256,64]{1,2,0:T(8,128)(2,1)} fusion(bf16[32,256,64]{1,2,0:T(8,128)(2,1)S(1)} %copy.113, s32[1024]{0:T(1024)S(1)} %pad_clamp_fusion.2), kind=kCustom, calls=%fused_computation.1 | custom fusion | bytes 12583680 | tf_op jit(solution)/shard_map/gather | solution.py:87
  99.7 18.3 %convolution_bitcast_fusion.1 = f32[192,256,64]{1,2,0:T(8,128)} fusion(bf16[192,256,64]{1,2,0:T(8,128)(2,1)} %gather_fusion.1, bf16[192,256,256]{2,1,0:T(8,128)(2,1)} %param.12), kind=kOutput, calls=%fused_computation.10 | convolution fusion | flops 1610612736 | bytes 44040192 | tf_op jit(solution)/shard_map/tij,tjc->tic/dot_general | solution.py:88
  118.1 16.9 %fusion.2 = f32[32,256,64]{1,0,2:T(8,128)} fusion(f32[192,256,64]{1,2,0:T(8,128)} %convolution_bitcast_fusion.1, s32[192]{0:T(256)S(1)} %bitcast.98, pred[192]{0:T(512)(128)(4,1)S(1)} %iota_compare_fusion.3), kind=kOutput, calls=%fused_computation.7 | convolution fusion | flops 1207971840 | bytes 14681024 | tf_op jit(solution)/shard_map/rt,tic->ric/dot_general | solution.py:89
  134.9 2.2 reshape.175
  137.1 2.1 fusion.12
  139.3 3.6 all-to-all-start.1
  143.1 3.0 fusion.40
  146.2 11.1 %all-to-all-done.1 = bf16[4,2048,64]{1,2,0:T(8,128)(2,1)S(1)} async-done(((bf16[4,2048,64]{1,2,0:T(8,128)(2,1)}), bf16[4,2048,64]{1,2,0:T(8,128)(2,1)S(1)}, u32[]{:S(2)}, u32[]{:S(2)}) %all-to-all-start.1) | async-done | bytes 1048608 | tf_op jit(solution)/shard_map/all_to_all | solution.py:94
  157.3 3.7 multiply_convert_fusion
  161.0 1.0 copy-done.6
  163.1 37.2 %all-reduce = (f32[]{:T(128)}, f32[]{:T(128)}) all-reduce(f32[]{:T(128)} %get-tuple-element.33, f32[]{:T(128)} %get-tuple-element.32), channel_id=1, replica_groups=mesh['grp'=8,'col'=4] {'grp','col'}, use_global_device_ids=true, to_apply=%region_5.6 | all-reduce | flops 2 | bytes 16 | tf_op jit(solution)/shard_map/psum | solution.py:153
  200.4 3.4 fusion.39
  203.8 1.4 fusion.10
  205.2 3.5 all-to-all-start.2
  208.8 14.4 %all-to-all-done.2 = bf16[2048,4,64]{0,2,1:T(8,128)(2,1)S(1)} async-done(((bf16[2048,4,64]{0,2,1:T(8,128)(2,1)}), bf16[2048,4,64]{0,2,1:T(8,128)(2,1)S(1)}, u32[]{:S(2)}, u32[]{:S(2)}) %all-to-all-start.2) | async-done | bytes 1048608 | tf_op jit(solution)/shard_map/all_to_all | solution.py:120
  223.2 1.8 copy.120
  225.0 2.6 reshape.176
  227.6 1.8 copy.121
  229.4 8.0 %gather_fusion.2 = bf16[192,256,64]{1,2,0:T(8,128)(2,1)} fusion(bf16[32,256,64]{1,2,0:T(8,128)(2,1)S(1)} %copy.121, s32[1024]{0:T(1024)S(1)} %pad_clamp_fusion.1), kind=kCustom, calls=%fused_computation.2 | custom fusion | bytes 12583680 | tf_op jit(solution)/shard_map/gather | solution.py:121
  237.3 19.0 %convolution_bitcast_fusion = f32[192,256,64]{1,2,0:T(8,128)} fusion(bf16[192,256,64]{1,2,0:T(8,128)(2,1)} %gather_fusion.2, bf16[192,256,256]{2,1,0:T(8,128)(2,1)} %param.12), kind=kOutput, calls=%fused_computation.9 | convolution fusion | flops 1610612736 | bytes 44040192 | tf_op jit(solution)/shard_map/tij,tic->tjc/dot_general | solution.py:122
  256.3 16.4 %fusion.13 = bf16[32,256,64]{1,0,2:T(8,128)(2,1)} fusion(f32[192,256,64]{1,2,0:T(8,128)} %convolution_bitcast_fusion, s32[192]{0:T(256)S(1)} %bitcast.97, pred[192]{0:T(512)(128)(4,1)S(1)} %iota_compare_fusion.3), kind=kOutput, calls=%fused_computation.30 | convolution fusion | flops 1208496128 | bytes 13632448 | tf_op jit(solution)/shard_map/rt,tjc->rjc/dot_general | solution.py:128
  272.8 1.9 convert_element_type.78
  274.6 1.6 copy.123
  276.2 3.5 all-to-all-start.3
  279.8 3.2 convolution_convert_fusion.3
  283.4 1.7 convolution_convert_fusion.1
  285.1 9.0 %all-to-all-done.3 = bf16[4,2048,64]{1,2,0:T(8,128)(2,1)S(1)} async-done(((bf16[4,2048,64]{1,2,0:T(8,128)(2,1)}), bf16[4,2048,64]{1,2,0:T(8,128)(2,1)S(1)}, u32[]{:S(2)}, u32[]{:S(2)}) %all-to-all-start.3) | async-done | bytes 1048608 | tf_op jit(solution)/shard_map/all_to_all | solution.py:131
  294.4 1.3 copy-done.18
  295.7 1.2 fusion.38
  297.7 1.0 copy.138
  298.7 21.9 %reduce-scatter.4.cloned.1.call-done = bf16[64,834]{1,0:T(8,128)(2,1)} async-done(((bf16[256,834]{1,0:T(8,128)(2,1)}), bf16[64,834]{1,0:T(8,128)(2,1)}) %reduce-scatter.4.cloned.1.call-update) | async-done | bytes 106768
  320.6 1.1 copy.139
  321.7 0.9 copy.125
  324.5 44.7 %all-gather.5.cloned.1.call-done = f32[8,834,64]{1,2,0:T(8,128)} async-done(((f32[1,834,64]{1,2,0:T(8,128)}), f32[8,834,64]{1,2,0:T(8,128)}) %all-gather.5.cloned.1.call-update) | async-done | bytes 1708048 | tf_op jit(solution)/shard_map/all_gather | solution.py:162
  369.2 1.6 reduce_sum.69
  (90 shorter events, 9.6 us)
Async XLA Ops:
  7.2 59.5 %copy-start = (bf16[2048,256]{1,0:T(8,128)(2,1)S(1)}, bf16[2048,256]{1,0:T(8,128)(2,1)}, u32[]{:S(2)}) copy-start(bf16[2048,256]{1,0:T(8,128)(2,1)} %param.11) | copy-start | bytes 3145732
  55.0 3.2 copy-start.15
  65.1 4.1 %copy-start.4 = (bf16[417,2,256]{2,1,0:T(2,128)(2,1)}, bf16[417,2,256]{2,1,0:T(2,128)(2,1)S(1)}, u32[]{:S(2)}) copy-start(bf16[417,2,256]{2,1,0:T(2,128)(2,1)S(1)} %gather_fusion) | copy-start | bytes 1281028
  69.2 4.6 %copy-start.11 = (s32[8192]{0:T(1024)S(1)}, s32[8192]{0:T(1024)}, u32[]{:S(2)}) copy-start(s32[8192]{0:T(1024)} %param.15) | copy-start | bytes 98308
  69.2 4.7 %copy-start.16 = (s32[1,192,2]{1,2,0:T(2,128)S(1)}, s32[1,192,2]{1,2,0:T(2,128)}, u32[]{:S(2)}) copy-start(s32[1,192,2]{1,2,0:T(2,128)} %param.13) | copy-start | bytes 4612
  69.2 18.3 %all-to-all-start = ((bf16[2048,4,64]{0,2,1:T(8,128)(2,1)}), bf16[2048,4,64]{0,2,1:T(8,128)(2,1)S(1)}, u32[]{:S(2)}, u32[]{:S(2)}) async-start(bf16[2048,4,64]{0,2,1:T(8,128)(2,1)} %bitcast.8), calls=%async_computation | async-start | bytes 2097152 | tf_op jit(solution)/shard_map/all_to_all | solution.py:78
  73.9 13.7 %copy-start.8 = (f32[8192]{0:T(1024)}, f32[8192]{0:T(1024)S(1)}, u32[]{:S(2)}) copy-start(f32[8192]{0:T(1024)S(1)} %convert_element_type.70) | copy-start | bytes 98308
  139.2 3.8 slice-start
  139.2 3.8 copy-start.12
  139.3 18.1 %all-to-all-start.1 = ((bf16[4,2048,64]{1,2,0:T(8,128)(2,1)}), bf16[4,2048,64]{1,2,0:T(8,128)(2,1)S(1)}, u32[]{:S(2)}, u32[]{:S(2)}) async-start(bf16[4,2048,64]{1,2,0:T(8,128)(2,1)} %fusion.12), calls=%async_computation.1 | async-start | bytes 2097152 | tf_op jit(solution)/shard_map/all_to_all | solution.py:94
  142.9 14.4 %copy-start.17 = (f32[1,256]{1,0:T(1,128)S(1)}, f32[1,256]{1,0:T(1,128)}, u32[]{:S(2)}) copy-start(f32[1,256]{1,0:T(1,128)} %get-tuple-element.39) | copy-start | bytes 3076
  157.3 5.0 %copy-start.14 = (s32[2048]{0:T(1024)S(1)}, s32[2048]{0:T(1024)}, u32[]{:S(2)}) copy-start(s32[2048]{0:T(1024)} %param.16) | copy-start | bytes 24580
  161.0 1.0 copy-start.6
  162.3 41.4 %copy-start.5 = (f32[2048,64]{0,1:T(8,128)}, f32[2048,64]{0,1:T(8,128)S(1)}, u32[]{:S(2)}) copy-start(f32[2048,64]{0,1:T(8,128)S(1)} %get-tuple-element.55) | copy-start | bytes 1572868
  200.4 3.4 dynamic-slice-start
  203.8 1.5 copy-start.1
  205.2 18.0 %all-to-all-start.2 = ((bf16[2048,4,64]{0,2,1:T(8,128)(2,1)}), bf16[2048,4,64]{0,2,1:T(8,128)(2,1)S(1)}, u32[]{:S(2)}, u32[]{:S(2)}) async-start(bf16[2048,4,64]{0,2,1:T(8,128)(2,1)} %bitcast.95), calls=%async_computation.2 | async-start | bytes 2097152 | tf_op jit(solution)/shard_map/all_to_all | solution.py:120
  276.2 17.9 %all-to-all-start.3 = ((bf16[4,2048,64]{1,2,0:T(8,128)(2,1)}), bf16[4,2048,64]{1,2,0:T(8,128)(2,1)S(1)}, u32[]{:S(2)}, u32[]{:S(2)}) async-start(bf16[4,2048,64]{1,2,0:T(8,128)(2,1)} %copy.123), calls=%async_computation.3 | async-start | bytes 2097152 | tf_op jit(solution)/shard_map/all_to_all | solution.py:131
  279.7 40.9 %reduce-scatter.4.cloned.1.call-start = ((), (), s32[]{:S(2)}) async-start(), calls=%async_computation.6 | async-start | bytes 573440
  279.7 3.2 copy-start.2
  285.1 9.2 %copy-start.3 = (bf16[2048,256]{0,1:T(8,128)(2,1)S(1)}, bf16[2048,256]{0,1:T(8,128)(2,1)}, u32[]{:S(2)}) copy-start(bf16[2048,256]{0,1:T(8,128)(2,1)} %copy-done.1) | copy-start | bytes 3145732
  294.1 1.6 copy-start.18
  296.9 0.8 copy-start.13
  297.4 25.2 %copy-start.7 = (f32[79,2,64]{0,2,1:T(8,128)S(1)}, f32[79,2,64]{0,2,1:T(8,128)}, u32[]{:S(2)}) copy-start(f32[79,2,64]{0,2,1:T(8,128)} %param.19) | copy-start | bytes 121348
  297.6 25.1 %copy-start.9 = (f32[79,2,64]{0,2,1:T(8,128)S(1)}, f32[79,2,64]{0,2,1:T(8,128)}, u32[]{:S(2)}) copy-start(f32[79,2,64]{0,2,1:T(8,128)} %param.20) | copy-start | bytes 121348
  297.6 25.3 %copy-start.10 = (f32[79,2,64]{0,2,1:T(8,128)S(1)}, f32[79,2,64]{0,2,1:T(8,128)}, u32[]{:S(2)}) copy-start(f32[79,2,64]{0,2,1:T(8,128)} %param.21) | copy-start | bytes 121348
  298.7 70.5 %all-gather.5.cloned.1.call-start = ((), (), s32[]{:S(2)}) async-start(), calls=%async_computation.5 | async-start | bytes 2064384 | tf_op jit(solution)/shard_map/all_gather | solution.py:162
Sparse Core Ops, SparseCore 0:
  298.8 21.7 reduce-scatter.3
  322.8 46.3 all-gather.4
